TPU v7x, 256 devices: a 8x8x2 block of a 8x8x16 slice. The times are simulated.
256 devices in a mesh: groups: 2 (over z), roll: 16 (over y, core), rows: 8 (over x).
Axes of the slice: x: 8, y: 8, z: 2, core: 2. Of those that a mesh axis runs over, the one named last changes fastest.
The devices are a block of a 8x8x16 slice.
Arguments:
- latent_slabs: bfloat16 [64, 3, 64, 8, 16], P(('groups', 'roll'), None, 'rows'), parts along dimension 0, may hold values from -18 to 18, as said below
- prior_latents: bfloat16 [64, 2, 64, 8, 16], P(('groups', 'roll'), None, 'rows'), parts along dimension 0, may hold values from -6 to 6
- prior_features: bfloat16 [64, 2, 64, 8, 512], P(('groups', 'roll'), None, 'rows'), parts along dimension 0, may hold values from -6 to 6
- lengths: int32 [64], P(('groups', 'roll')), parts along dimension 0, may hold values from 1 to 3
- starts: int32 [64], P(('groups', 'roll')), parts along dimension 0, may hold values from 0 to 6, as said below
- move_plan: int32 [64], P(('groups', 'roll')), parts along dimension 0, may hold values from -1 to 15, as said below
- entry_weight: bfloat16 [432, 512], replicated, may hold values from -0.3125 to 0.3125
- block_weight: bfloat16 [13824, 512], P(None, ('roll', 'rows')), may hold values from -0.0546875 to 0.0546875
- norm_gain: float32 [512], replicated, may hold values from 0.25 to 1.75
- norm_shift: float32 [512], replicated, may hold values from -1.2 to 1.2
Outputs:
- decoded: bfloat16 [64, 3, 64, 8, 512], P(('groups', 'roll'), None, 'rows'), parts along dimension 0
There are 2 independent parts, one for each index of `groups`. A program takes and returns all parts, laid end to end along the dimension named above; an argument that names none is the same for every part. Nothing has to cross between parts.
Inputs may be any that keep to these rules, and one draw needn't show every extreme that they name: `latent_slabs`: normal or uniform values times a scale that varies over the rows. `starts`: multiples of 3. `move_plan`: A value d * 1 + c names compute slot c of roll index d. Every compute slot of the part is named by exactly one slab, and the slabs held by one roll index name at most 1 slots of any one roll index.
All inputs are finite; a program needn't handle non-finite values.
Results may differ from a plain program's by a relative error of at most 0.0023.
Values may be sent and summed in bfloat16 or wider, within the bound.
No kernel may reach another device: no remote copies, remote signals or barrier semaphores. Data moves between devices by JAX's collectives and lax.ppermute only.
A program may use at most 128 MiB of HBM per device.

v0:
```python
import jax
import jax.numpy as jnp
from jax import lax
from jax.sharding import PartitionSpec as P

GROUPS = 32
EPSILON = 1e-06


def padded(x, sides, width):
    for axis, dim in sides:
        count, length = (lax.axis_size(axis), x.shape[dim])
        up = [(i, (i + 1) % count) for i in range(count - 1)]
        down = [(j, i) for i, j in up]
        last = lax.slice_in_dim(x, length - width, length, axis=dim)
        first = lax.slice_in_dim(x, 0, width, axis=dim)
        before = lax.ppermute(last, axis, up)
        after = lax.ppermute(first, axis, down)
        x = jnp.concatenate([before, x, after], axis=dim)
    return x


def column_pad(extended):
    return jnp.pad(extended, ((0, 0), (0, 0), (0, 0), (1, 1), (0, 0)))


def convolve(extended, weights):
    slots = extended.shape[0]
    frames = extended.shape[1] - 2
    height = extended.shape[2] - 2
    widths = extended.shape[3] - 2
    channels = extended.shape[4]
    accumulated = jnp.zeros((slots * frames * height * widths, weights.shape[1]), jnp.float32)
    for tap_index in range(27):
        step_t = tap_index // 9
        step_h = tap_index // 3 % 3
        step_w = tap_index % 3
        window = extended[
            :, step_t : step_t + frames, step_h : step_h + height, step_w : step_w + widths, :
        ]
        accumulated = accumulated + jnp.dot(
            window.reshape(-1, channels),
            weights[tap_index * channels : (tap_index + 1) * channels],
            preferred_element_type=jnp.float32,
        )
    return accumulated.reshape(slots, frames, height, widths, weights.shape[1])


def decode(
    entry_ext, feature_cache, live_lengths, entry_weight, block_weight, norm_gain, norm_shift
):
    latent_rim = padded(entry_ext, (("rows", 2),), 1)
    hidden = convolve(column_pad(latent_rim), entry_weight)
    slots, frames, height, widths, features = hidden.shape
    grouped = hidden.reshape(slots, frames, height, widths, GROUPS, features // GROUPS)
    group_sums = jnp.sum(grouped, axis=(2, 3, 5))
    squares = jnp.sum(grouped * grouped, axis=(2, 3, 5))
    group_sums, squares = lax.psum((group_sums, squares), "rows")
    cell_count = height * lax.axis_size("rows") * widths * (features // GROUPS)
    group_mean = group_sums / cell_count
    spread = squares / cell_count - group_mean * group_mean
    scaled = lax.rsqrt(spread + EPSILON)
    normed = (
        (grouped - group_mean[:, :, None, None, :, None]) * scaled[:, :, None, None, :, None]
    ).reshape(hidden.shape)
    normed = normed * norm_gain + norm_shift
    active = jax.nn.silu(normed).astype(jnp.bfloat16)
    stacked = jnp.concatenate([feature_cache, active], axis=1)
    bordered = column_pad(padded(stacked, (("rows", 2),), 1))
    mixed_sum = convolve(
        bordered, lax.all_gather(block_weight, ("roll", "rows"), axis=1, tiled=True)
    )
    alive_frames = jnp.arange(frames)[None, :] < live_lengths[:, None]
    return jnp.where(alive_frames[:, :, None, None, None], hidden + mixed_sum, 0.0).astype(
        jnp.bfloat16
    )


def on_device(
    latent_slabs,
    prior_latents,
    prior_features,
    lengths,
    starts,
    move_plan,
    entry_weight,
    block_weight,
    norm_gain,
    norm_shift,
):
    cached = starts > 0
    prior_lat = jnp.where(
        cached[:, None, None, None, None], prior_latents, jnp.zeros_like(prior_latents)
    )
    feature_cache = jnp.where(
        cached[:, None, None, None, None], prior_features, jnp.zeros_like(prior_features)
    )
    entry_ext = jnp.concatenate([prior_lat, latent_slabs], axis=1)
    live_lengths = jnp.where(move_plan >= 0, lengths, 0)
    return decode(
        entry_ext, feature_cache, live_lengths, entry_weight, block_weight, norm_gain, norm_shift
    )


def solution(mesh):
    in_specs = (
        P(("groups", "roll"), None, "rows", None, None),
        P(("groups", "roll"), None, "rows", None, None),
        P(("groups", "roll"), None, "rows", None, None),
        P(("groups", "roll")),
        P(("groups", "roll")),
        P(("groups", "roll")),
        P(),
        P(None, ("roll", "rows")),
        P(),
        P(),
    )
    out_specs = P(("groups", "roll"), None, "rows", None, None)
    return jax.shard_map(
        on_device, mesh=mesh, in_specs=in_specs, out_specs=out_specs, check_vma=False
    )
```

profile of v0, /device:TPU:513, one launch (start us, length us, event | category | flops | bytes accessed | tf_op | source)
XLA Modules:
  0.0 172.0 jit_solution(16088518740461033009)
XLA Ops:
  9.6 1.3 collective-permute-start.1
  10.9 4.7 %collective-permute-start = (bf16[2,5,1,8,16]{4,3,2,1,0:T(8,128)(2,1)S(1)}, bf16[2,5,1,8,16]{4,3,2,1,0:T(8,128)(2,1)S(1)}, u32[]{:S(2)}, u32[]{:S(2)}) collective-permute-start(bf16[2,5,1,8,16]{4,3,2,1,0:T(8,128)(2,1)S(1)} %get-tuple-element.67), channel_id=1, source_target_pairs={{0,1},{1,2},{2,3},{3,4},{4,5},{5,6},{6,7},{8,9},{9,10},{10,11},{11... | collective-permute-start | bytes 7688 | tf_op jit(solution)/shard_map/ppermute | solution.py:17
  16.4 1.0 broadcast_select_fusion
  18.4 1.1 pad_maximum_fusion.2
  19.5 1.1 select_maximum_fusion.2
  21.0 1.0 fusion.98
  21.9 0.9 convolution_add_fusion.33
  22.9 0.9 convolution_add_fusion.32
  23.8 1.0 convolution_add_fusion.31
  24.8 1.0 convolution_add_fusion.30
  31.0 4.1 %reshape_reshape.3 = f32[2,3,8,8,32,16]{5,4,3,2,1,0:T(8,128)} reshape(f32[384,512]{1,0:T(8,128)S(1)} %convolution_add_fusion.8) | data formatting | bytes 1572864 | tf_op jit(solution)/shard_map/reshape;reshape | solution.py:55
  35.1 4.0 %fusion.100 = (f32[2,3,32]{2,1,0:T(4,128)S(1)}, f32[2,3,32]{2,1,0:T(4,128)S(1)}) fusion(f32[2,3,8,8,32,16]{5,4,3,2,1,0:T(8,128)} %reshape_reshape.3), kind=kLoop, calls=%fused_computation.169 | loop fusion | flops 589440 | bytes 787968 | tf_op jit(solution)/shard_map/reduce_sum | solution.py:56
  39.1 14.4 %all-reduce.2 = (f32[2,3,32]{2,1,0:T(4,128)S(1)}, f32[2,3,32]{2,1,0:T(4,128)S(1)}) all-reduce(f32[2,3,32]{2,1,0:T(4,128)S(1)} %get-tuple-element.6, f32[2,3,32]{2,1,0:T(4,128)S(1)} %get-tuple-element.5), channel_id=1, replica_groups=mesh['groups'=2,'roll'=16,'rows'=8] {'rows'}, use_global_device_ids=true, to_apply=%region_3.4 | all-reduce | flops 384 | bytes 3072 | tf_op jit(solution)/shard_map/psum | solution.py:58
  54.0 1.0 multiply_convert_fusion
  55.3 2.2 %collective-permute-start.2 = (bf16[2,5,1,8,512]{4,3,2,1,0:T(8,128)(2,1)S(1)}, bf16[2,5,1,8,512]{4,3,2,1,0:T(8,128)(2,1)S(1)}, u32[]{:S(2)}, u32[]{:S(2)}) collective-permute-start(bf16[2,5,1,8,512]{4,3,2,1,0:T(8,128)(2,1)S(1)} %get-tuple-element.37), channel_id=1, source_target_pairs={{0,1},{1,2},{2,3},{3,4},{4,5},{5,6},{6,7},{8,9},{9,10},{10,11},{11... | collective-permute-start | bytes 245768 | tf_op jit(solution)/shard_map/ppermute | solution.py:17
  57.5 1.5 collective-permute-start.3
  59.0 0.9 fusion.70
  60.0 3.6 %collective-permute-done.3 = bf16[2,5,1,8,512]{4,3,2,1,0:T(8,128)(2,1)S(1)} collective-permute-done((bf16[2,5,1,8,512]{4,3,2,1,0:T(8,128)(2,1)S(1)}, bf16[2,5,1,8,512]{4,3,2,1,0:T(8,128)(2,1)S(1)}, u32[]{:S(2)}, u32[]{:S(2)}) %collective-permute-start.3) | collective-permute-done | bytes 81952 | tf_op jit(solution)/shard_map/ppermute | solution.py:18
  63.7 1.0 fusion.103
  64.8 1.1 fusion.102
  66.8 2.5 %fusion.101 = (bf16[2,3,8,8,512]{4,3,2,1,0:T(8,128)(2,1)S(1)}, bf16[2,3,8,8,512]{4,3,2,1,0:T(8,128)(2,1)}, bf16[2,3,8,8,512]{4,3,2,1,0:T(8,128)(2,1)}, bf16[2,3,...) fusion(bf16[2,5,10,10,512]{4,3,2,1,0:T(8,128)(2,1)S(1)} %select, ...), kind=kLoop, calls=%fused_computation.170 | loop fusion | bytes 14155776 | tf_op jit(solution)/shard_map/slice | solution.py:38
  69.3 51.0 %all-gather.3.cloned.1.call-done = bf16[128,4,13824]{2,1,0:T(4,128)(2,1)} async-done(((bf16[1,4,13824]{2,1,0:T(4,128)(2,1)}), bf16[128,4,13824]{2,1,0:T(4,128)(2,1)}) %all-gather.3.cloned.1.call-update) | async-done | bytes 14155792 | tf_op jit(solution)/shard_map/all_gather | solution.py:71
  120.3 20.3 %reshape.254 = bf16[512,13824]{1,0:T(8,128)(2,1)} reshape(bf16[128,4,13824]{2,1,0:T(4,128)(2,1)} %all-gather.3.cloned.1.call-done) | data formatting | bytes 28311552
  140.7 1.7 fusion.22
  142.4 2.3 %fusion.24 = f32[384,512]{1,0:T(8,128)S(1)} fusion(bf16[384,512]{1,0:T(8,128)(2,1)} %bitcast.177, bf16[13824,512]{0,1:T(8,128)(2,1)} %bitcast.136), kind=kOutput, calls=%fused_computation.74 | convolution fusion | flops 201326592 | bytes 1703936 | tf_op jit(solution)/shard_map/dot_general | solution.py:41
  144.7 2.3 %fusion.27 = f32[384,512]{1,0:T(8,128)S(1)} fusion(bf16[384,512]{1,0:T(8,128)(2,1)} %multiply_convert_fusion, bf16[13824,512]{0,1:T(8,128)(2,1)} %bitcast.137), kind=kOutput, calls=%fused_computation.77 | convolution fusion | flops 201326592 | bytes 1703936 | tf_op jit(solution)/shard_map/dot_general | solution.py:41
  147.0 1.6 fusion.29
  148.6 1.6 fusion.32
  150.2 1.6 fusion.34
  151.7 1.6 fusion.37
  153.3 1.6 fusion.39
  154.9 1.6 fusion.42
  (99 shorter events, 20.3 us)
Async XLA Ops:
  6.5 19.2 %copy-start.13 = (bf16[432,512]{1,0:T(8,128)(2,1)S(1)}, bf16[432,512]{1,0:T(8,128)(2,1)}, u32[]{:S(2)}) copy-start(bf16[432,512]{1,0:T(8,128)(2,1)} %param.16) | copy-start | bytes 1327108
  6.5 113.8 %all-gather.3.cloned.1.call-start = ((), (), s32[]{:S(2)}) async-start(), calls=%async_computation | async-start | bytes 14266368 | tf_op jit(solution)/shard_map/all_gather | solution.py:71
  9.6 8.8 %collective-permute-start.1 = (bf16[2,5,1,8,16]{4,3,2,1,0:T(8,128)(2,1)S(1)}, bf16[2,5,1,8,16]{4,3,2,1,0:T(8,128)(2,1)S(1)}, u32[]{:S(2)}, u32[]{:S(2)}) collective-permute-start(bf16[2,5,1,8,16]{4,3,2,1,0:T(8,128)(2,1)S(1)} %get-tuple-element.68), channel_id=1, source_target_pairs={{1,0},{2,1},{3,2},{4,3},{5,4},{6,5},{7,6},{9,8},{10,9},{11,10},{12... | collective-permute-start | bytes 7688 | tf_op jit(solution)/shard_map/ppermute | solution.py:18
  10.9 7.4 %collective-permute-start = (bf16[2,5,1,8,16]{4,3,2,1,0:T(8,128)(2,1)S(1)}, bf16[2,5,1,8,16]{4,3,2,1,0:T(8,128)(2,1)S(1)}, u32[]{:S(2)}, u32[]{:S(2)}) collective-permute-start(bf16[2,5,1,8,16]{4,3,2,1,0:T(8,128)(2,1)S(1)} %get-tuple-element.67), channel_id=1, source_target_pairs={{0,1},{1,2},{2,3},{3,4},{4,5},{5,6},{6,7},{8,9},{9,10},{10,11},{11... | collective-permute-start | bytes 7688 | tf_op jit(solution)/shard_map/ppermute | solution.py:17
  25.8 4.0 %copy-start.1 = (bf16[2,3,8,8,16]{4,3,2,1,0:T(8,128)(2,1)S(1)}, bf16[2,3,8,8,16]{4,3,2,1,0:T(8,128)(2,1)}, u32[]{:S(2)}) copy-start(bf16[2,3,8,8,16]{4,3,2,1,0:T(8,128)(2,1)} %param.10) | copy-start | bytes 36868
  28.8 25.2 %copy-start.14 = (f32[512]{0:T(512)S(1)}, f32[512]{0:T(512)}, u32[]{:S(2)}) copy-start(f32[512]{0:T(512)} %param.19) | copy-start | bytes 6148
  28.8 25.2 %copy-start.15 = (f32[512]{0:T(512)S(1)}, f32[512]{0:T(512)}, u32[]{:S(2)}) copy-start(f32[512]{0:T(512)} %param.18) | copy-start | bytes 6148
  55.3 4.6 %collective-permute-start.2 = (bf16[2,5,1,8,512]{4,3,2,1,0:T(8,128)(2,1)S(1)}, bf16[2,5,1,8,512]{4,3,2,1,0:T(8,128)(2,1)S(1)}, u32[]{:S(2)}, u32[]{:S(2)}) collective-permute-start(bf16[2,5,1,8,512]{4,3,2,1,0:T(8,128)(2,1)S(1)} %get-tuple-element.37), channel_id=1, source_target_pairs={{0,1},{1,2},{2,3},{3,4},{4,5},{5,6},{6,7},{8,9},{9,10},{10,11},{11... | collective-permute-start | bytes 245768 | tf_op jit(solution)/shard_map/ppermute | solution.py:17
  57.5 6.1 %collective-permute-start.3 = (bf16[2,5,1,8,512]{4,3,2,1,0:T(8,128)(2,1)S(1)}, bf16[2,5,1,8,512]{4,3,2,1,0:T(8,128)(2,1)S(1)}, u32[]{:S(2)}, u32[]{:S(2)}) collective-permute-start(bf16[2,5,1,8,512]{4,3,2,1,0:T(8,128)(2,1)S(1)} %get-tuple-element.38), channel_id=1, source_target_pairs={{1,0},{2,1},{3,2},{4,3},{5,4},{6,5},{7,6},{9,8},{10,9},{11,10},{12... | collective-permute-start | bytes 245768 | tf_op jit(solution)/shard_map/ppermute | solution.py:18
  140.6 15.8 %copy-start = (bf16[512,13824]{1,0:T(8,128)(2,1)S(1)}, bf16[512,13824]{1,0:T(8,128)(2,1)}, u32[]{:S(2)}) copy-start(bf16[512,13824]{1,0:T(8,128)(2,1)} %reshape.254) | copy-start | bytes 42467332
  140.6 15.8 %copy-start.2 = (bf16[2,3,8,8,512]{4,3,2,1,0:T(8,128)(2,1)S(1)}, bf16[2,3,8,8,512]{4,3,2,1,0:T(8,128)(2,1)}, u32[]{:S(2)}) copy-start(bf16[2,3,8,8,512]{4,3,2,1,0:T(8,128)(2,1)} %get-tuple-element.18) | copy-start | bytes 1179652
  140.6 16.3 %copy-start.11 = (bf16[2,3,8,8,512]{4,3,2,1,0:T(8,128)(2,1)S(1)}, bf16[2,3,8,8,512]{4,3,2,1,0:T(8,128)(2,1)}, u32[]{:S(2)}) copy-start(bf16[2,3,8,8,512]{4,3,2,1,0:T(8,128)(2,1)} %get-tuple-element.29) | copy-start | bytes 1179652
  140.6 17.1 %copy-start.10 = (bf16[2,3,8,8,512]{4,3,2,1,0:T(8,128)(2,1)S(1)}, bf16[2,3,8,8,512]{4,3,2,1,0:T(8,128)(2,1)}, u32[]{:S(2)}) copy-start(bf16[2,3,8,8,512]{4,3,2,1,0:T(8,128)(2,1)} %get-tuple-element.30) | copy-start | bytes 1179652
  140.7 17.9 %copy-start.12 = (bf16[2,3,8,8,512]{4,3,2,1,0:T(8,128)(2,1)S(1)}, bf16[2,3,8,8,512]{4,3,2,1,0:T(8,128)(2,1)}, u32[]{:S(2)}) copy-start(bf16[2,3,8,8,512]{4,3,2,1,0:T(8,128)(2,1)} %get-tuple-element.33) | copy-start | bytes 1179652
  142.4 17.8 %copy-start.9 = (bf16[2,3,8,8,512]{4,3,2,1,0:T(8,128)(2,1)S(1)}, bf16[2,3,8,8,512]{4,3,2,1,0:T(8,128)(2,1)}, u32[]{:S(2)}) copy-start(bf16[2,3,8,8,512]{4,3,2,1,0:T(8,128)(2,1)} %get-tuple-element.27) | copy-start | bytes 1179652
  153.3 7.9 %copy-start.8 = (bf16[2,3,8,8,512]{4,3,2,1,0:T(8,128)(2,1)S(1)}, bf16[2,3,8,8,512]{4,3,2,1,0:T(8,128)(2,1)}, u32[]{:S(2)}) copy-start(bf16[2,3,8,8,512]{4,3,2,1,0:T(8,128)(2,1)} %get-tuple-element.21) | copy-start | bytes 1179652
  156.5 5.1 %copy-start.7 = (bf16[2,3,8,8,512]{4,3,2,1,0:T(8,128)(2,1)S(1)}, bf16[2,3,8,8,512]{4,3,2,1,0:T(8,128)(2,1)}, u32[]{:S(2)}) copy-start(bf16[2,3,8,8,512]{4,3,2,1,0:T(8,128)(2,1)} %get-tuple-element.19) | copy-start | bytes 1179652
  157.3 4.7 %copy-start.6 = (bf16[2,3,8,8,512]{4,3,2,1,0:T(8,128)(2,1)S(1)}, bf16[2,3,8,8,512]{4,3,2,1,0:T(8,128)(2,1)}, u32[]{:S(2)}) copy-start(bf16[2,3,8,8,512]{4,3,2,1,0:T(8,128)(2,1)} %get-tuple-element.17) | copy-start | bytes 1179652
  158.5 3.9 %copy-start.5 = (bf16[2,3,8,8,512]{4,3,2,1,0:T(8,128)(2,1)S(1)}, bf16[2,3,8,8,512]{4,3,2,1,0:T(8,128)(2,1)}, u32[]{:S(2)}) copy-start(bf16[2,3,8,8,512]{4,3,2,1,0:T(8,128)(2,1)} %get-tuple-element.15) | copy-start | bytes 1179652
  159.4 3.6 %copy-start.4 = (bf16[2,3,8,8,512]{4,3,2,1,0:T(8,128)(2,1)S(1)}, bf16[2,3,8,8,512]{4,3,2,1,0:T(8,128)(2,1)}, u32[]{:S(2)}) copy-start(bf16[2,3,8,8,512]{4,3,2,1,0:T(8,128)(2,1)} %get-tuple-element.13) | copy-start | bytes 1179652
  160.6 2.8 %copy-start.3 = (bf16[2,3,8,8,512]{4,3,2,1,0:T(8,128)(2,1)S(1)}, bf16[2,3,8,8,512]{4,3,2,1,0:T(8,128)(2,1)}, u32[]{:S(2)}) copy-start(bf16[2,3,8,8,512]{4,3,2,1,0:T(8,128)(2,1)} %get-tuple-element.11) | copy-start | bytes 1179652
Sparse Core Ops, SparseCore 0:
  10.0 110.3 all-gather.2
where the time goes:
time: 173 us; the launch traced here: 172 us
  waiting for transfers between devices  55.4 us (32%)
  matrix products  32.9 us (19%)
  local copies, waits for them, and re-layouts  29.9 us (17%)
  other arithmetic  15.4 us (9%)
  blocking collectives  14.4 us (8%)
  between operations  14.2 us (8%)
  starting transfers between devices  9.74 us (6%)
    all_gather x1, waiting for transfers between devices, decode(): lax.all_gather(block_weight, ('roll', 'rows'), axis=1, tiled=True)  51 us
    dot_general x54, matrix products, convolve(): jnp.dot(window.reshape(-1, channels), weights[tap_index * channels:(tap_i...  32.9 us
    unnamed x33, local copies, waits for them, and re-layouts  20.4 us
    psum x1, blocking collectives, decode(): group_sums, squares = lax.psum((group_sums, squares), 'rows')  14.4 us
    ppermute x2, starting transfers between devices, padded(): before = lax.ppermute(last, axis, up)  6.94 us
    slice x5, local copies, waits for them, and re-layouts, convolve(): extended[:, step_t:step_t + frames, step_h:step_h + height, step_w:step_w...  5.04 us
    another operation x1, local copies, waits for them, and re-layouts, decode(): hidden.reshape(slots, frames, height, widths, GROUPS, features // GROUPS)  4.1 us
    reduce_sum x1, other arithmetic, decode(): group_sums = jnp.sum(grouped, axis=(2, 3, 5))  4.05 us
  transfers between devices with their start and end apart: 5, of which 2 were waited for; matrix products, arithmetic and copies ran while one was open for 20% of the time, Pallas kernels for 0%

commit v1 on v0

--- a/solution.py
+++ b/solution.py
@@ -68,7 +68,13 @@
     stacked = jnp.concatenate([feature_cache, active], axis=1)
     bordered = column_pad(padded(stacked, (("rows", 2),), 1))
     mixed_sum = convolve(
-        bordered, lax.all_gather(block_weight, ("roll", "rows"), axis=1, tiled=True)
+        bordered,
+        jnp.concatenate(
+            lax.all_to_all(
+                jnp.stack([block_weight] * lax.axis_size(("roll", "rows"))), ("roll", "rows"), 0, 0
+            ),
+            axis=1,
+        ),
     )
     alive_frames = jnp.arange(frames)[None, :] < live_lengths[:, None]
     return jnp.where(alive_frames[:, :, None, None, None], hidden + mixed_sum, 0.0).astype(

time: 173 us -> 608 us (3.51)
  the two profiles are of different devices: /device:TPU:513 before, /device:TPU:582 now
where the time goes in v1:
time: 608 us; the launch traced here: 607 us
  waiting for transfers between devices  397 us (65%)
  local copies, waits for them, and re-layouts  75.7 us (12%)
  blocking collectives  65.8 us (11%)
  starting transfers between devices  37.3 us (6%)
  matrix products  20.7 us (3%)
  other arithmetic  8.86 us (1%)
    ppermute x2, waiting for transfers between devices, padded(): before = lax.ppermute(last, axis, up)  388 us
    psum x1, blocking collectives, decode(): group_sums, squares = lax.psum((group_sums, squares), 'rows')  65.8 us
    slice x29, local copies, waits for them, and re-layouts, convolve(): weights[tap_index * channels:(tap_index + 1) * channels]  57.6 us
    all_to_all x1, starting transfers between devices, decode(): lax.all_to_all(jnp.stack([block_weight] * lax.axis_size(('roll', 'rows'))...  23.2 us
    dot_general x54, matrix products, convolve(): jnp.dot(window.reshape(-1, channels), weights[tap_index * channels:(tap_i...  20.7 us
  transfers between devices with their start and end apart: 5, of which 3 were waited for; matrix products, arithmetic and copies ran while one was open for 4% of the time, Pallas kernels for 0%

profile of v1, /device:TPU:582, one launch (start us, length us, event | category | flops | bytes accessed | tf_op | source)
XLA Modules:
  0.0 606.6 jit_solution(12398387337412590054)
XLA Ops:
  0.0 6.1 stack.2
  6.1 23.2 %all-to-all-start = ((bf16[128,13824,4]{1,2,0:T(4,128)(2,1)}), bf16[128,13824,4]{1,2,0:T(4,128)(2,1)}, u32[]{:S(2)}, u32[]{:S(2)}) async-start(bf16[128,13824,4]{1,2,0:T(4,128)(2,1)} %stack.2), calls=%async_computation | async-start | bytes 28311552 | tf_op jit(solution)/shard_map/all_to_all | solution.py:73
  29.4 4.6 collective-permute-start
  34.1 2.0 collective-permute-start.1
  36.3 387.7 %collective-permute-done = bf16[2,5,1,8,16]{4,3,2,1,0:T(8,128)(2,1)S(1)} collective-permute-done((bf16[2,5,1,8,16]{4,3,2,1,0:T(8,128)(2,1)S(1)}, bf16[2,5,1,8,16]{4,3,2,1,0:T(8,128)(2,1)S(1)}, u32[]{:S(2)}, u32[]{:S(2)}) %collective-permute-start) | collective-permute-done | bytes 2592 | tf_op jit(solution)/shard_map/ppermute | solution.py:17
  423.9 4.9 collective-permute-done.1
  435.8 4.1 reshape_reshape.3
  439.9 4.1 fusion.54
  443.9 65.8 %all-reduce.2 = (f32[2,3,32]{2,1,0:T(4,128)S(1)}, f32[2,3,32]{2,1,0:T(4,128)S(1)}) all-reduce(f32[2,3,32]{2,1,0:T(4,128)S(1)} %get-tuple-element.6, f32[2,3,32]{2,1,0:T(4,128)S(1)} %get-tuple-element.5), channel_id=1, replica_groups=mesh['groups'=2,'roll'=16,'rows'=8] {'rows'}, use_global_device_ids=true, to_apply=%region_3.4 | all-reduce | flops 384 | bytes 3072 | tf_op jit(solution)/shard_map/psum | solution.py:58
  511.6 5.4 collective-permute-start.2
  517.0 2.1 collective-permute-start.3
  520.1 4.5 collective-permute-done.3
  527.7 3.2 fusion.57
  530.9 4.0 fusion.56
  535.0 8.0 %fusion.55 = (bf16[512,128,4]{0,2,1:T(4,128)(2,1)S(1)}, bf16[512,128,4]{0,2,1:T(4,128)(2,1)S(1)}, bf16[512,128,4]{0,2,1:T(4,128)(2,1)S(1)}, bf16[512,128,4]{0,2,...) fusion(bf16[13824,128,4]{0,2,1:T(4,128)(2,1)} %bitcast.29), kind=kLoop, calls=%fused_computation.124 | loop fusion | bytes 19922944 | tf_op jit(solution)/shard_map/slice | solution.py:43
  543.0 2.0 slice.508
  545.0 2.0 slice.514
  547.0 2.0 slice.517
  548.9 2.0 slice.526
  550.9 2.0 slice.511
  552.9 2.0 slice.529
  556.9 2.0 slice.535
  560.9 2.0 slice.532
  564.8 2.0 slice.547
  568.8 2.0 slice.553
  572.7 2.0 slice.550
  574.7 2.0 slice.562
  576.6 2.0 slice.565
  578.6 2.0 slice.559
  580.6 2.0 slice.571
  582.5 2.0 slice.573
  584.5 2.0 slice.568
  (203 shorter events, 42.2 us)
Async XLA Ops:
  6.1 23.2 %copy-start.51 = (s32[2]{0:T(128)S(1)}, s32[2]{0:T(128)}, u32[]{:S(2)}) copy-start(s32[2]{0:T(128)} %param.14) | copy-start | bytes 28
  6.1 23.2 %copy-start.48 = (bf16[2,2,8,8,16]{4,3,2,1,0:T(8,128)(2,1)S(1)}, bf16[2,2,8,8,16]{4,3,2,1,0:T(8,128)(2,1)}, u32[]{:S(2)}) copy-start(bf16[2,2,8,8,16]{4,3,2,1,0:T(8,128)(2,1)} %param.11) | copy-start | bytes 24580
  6.1 23.3 %copy-start = (bf16[2,3,8,8,16]{4,3,2,1,0:T(8,128)(2,1)S(1)}, bf16[2,3,8,8,16]{4,3,2,1,0:T(8,128)(2,1)}, u32[]{:S(2)}) copy-start(bf16[2,3,8,8,16]{4,3,2,1,0:T(8,128)(2,1)} %param.10) | copy-start | bytes 36868
  6.1 29.9 %copy-start.52 = (s32[2]{0:T(128)S(1)}, s32[2]{0:T(128)}, u32[]{:S(2)}) copy-start(s32[2]{0:T(128)} %param.13) | copy-start | bytes 28
  6.1 29.9 %copy-start.53 = (s32[2]{0:T(128)S(1)}, s32[2]{0:T(128)}, u32[]{:S(2)}) copy-start(s32[2]{0:T(128)} %param.15) | copy-start | bytes 28
  6.1 30.0 %copy-start.47 = (bf16[2,2,8,8,512]{4,3,2,1,0:T(8,128)(2,1)S(1)}, bf16[2,2,8,8,512]{4,3,2,1,0:T(8,128)(2,1)}, u32[]{:S(2)}) copy-start(bf16[2,2,8,8,512]{4,3,2,1,0:T(8,128)(2,1)} %param.12) | copy-start | bytes 786436
  6.1 524.8 %all-to-all-start = ((bf16[128,13824,4]{1,2,0:T(4,128)(2,1)}), bf16[128,13824,4]{1,2,0:T(4,128)(2,1)}, u32[]{:S(2)}, u32[]{:S(2)}) async-start(bf16[128,13824,4]{1,2,0:T(4,128)(2,1)} %stack.2), calls=%async_computation | async-start | bytes 28311552 | tf_op jit(solution)/shard_map/all_to_all | solution.py:73
  29.4 394.5 %collective-permute-start = (bf16[2,5,1,8,16]{4,3,2,1,0:T(8,128)(2,1)S(1)}, bf16[2,5,1,8,16]{4,3,2,1,0:T(8,128)(2,1)S(1)}, u32[]{:S(2)}, u32[]{:S(2)}) collective-permute-start(bf16[2,5,1,8,16]{4,3,2,1,0:T(8,128)(2,1)S(1)} %get-tuple-element.94), channel_id=1, source_target_pairs={{0,1},{1,2},{2,3},{3,4},{4,5},{5,6},{6,7},{8,9},{9,10},{10,11},{11... | collective-permute-start | bytes 7688 | tf_op jit(solution)/shard_map/ppermute | solution.py:17
  34.1 394.7 %collective-permute-start.1 = (bf16[2,5,1,8,16]{4,3,2,1,0:T(8,128)(2,1)S(1)}, bf16[2,5,1,8,16]{4,3,2,1,0:T(8,128)(2,1)S(1)}, u32[]{:S(2)}, u32[]{:S(2)}) collective-permute-start(bf16[2,5,1,8,16]{4,3,2,1,0:T(8,128)(2,1)S(1)} %get-tuple-element.95), channel_id=1, source_target_pairs={{1,0},{2,1},{3,2},{4,3},{5,4},{6,5},{7,6},{9,8},{10,9},{11,10},{12... | collective-permute-start | bytes 7688 | tf_op jit(solution)/shard_map/ppermute | solution.py:18
  36.1 393.4 %copy-start.46 = (bf16[432,512]{1,0:T(8,128)(2,1)S(1)}, bf16[432,512]{1,0:T(8,128)(2,1)}, u32[]{:S(2)}) copy-start(bf16[432,512]{1,0:T(8,128)(2,1)} %param.16) | copy-start | bytes 1327108
  439.9 70.4 %copy-start.49 = (f32[512]{0:T(512)S(1)}, f32[512]{0:T(512)}, u32[]{:S(2)}) copy-start(f32[512]{0:T(512)} %param.19) | copy-start | bytes 6148
  439.9 70.4 %copy-start.50 = (f32[512]{0:T(512)S(1)}, f32[512]{0:T(512)}, u32[]{:S(2)}) copy-start(f32[512]{0:T(512)} %param.18) | copy-start | bytes 6148
  511.6 8.5 %collective-permute-start.2 = (bf16[2,5,1,8,512]{4,3,2,1,0:T(8,128)(2,1)S(1)}, bf16[2,5,1,8,512]{4,3,2,1,0:T(8,128)(2,1)S(1)}, u32[]{:S(2)}, u32[]{:S(2)}) collective-permute-start(bf16[2,5,1,8,512]{4,3,2,1,0:T(8,128)(2,1)S(1)} %get-tuple-element.64), channel_id=1, source_target_pairs={{0,1},{1,2},{2,3},{3,4},{4,5},{5,6},{6,7},{8,9},{9,10},{10,11},{11... | collective-permute-start | bytes 245768 | tf_op jit(solution)/shard_map/ppermute | solution.py:17
  517.0 7.6 %collective-permute-start.3 = (bf16[2,5,1,8,512]{4,3,2,1,0:T(8,128)(2,1)S(1)}, bf16[2,5,1,8,512]{4,3,2,1,0:T(8,128)(2,1)S(1)}, u32[]{:S(2)}, u32[]{:S(2)}) collective-permute-start(bf16[2,5,1,8,512]{4,3,2,1,0:T(8,128)(2,1)S(1)} %get-tuple-element.65), channel_id=1, source_target_pairs={{1,0},{2,1},{3,2},{4,3},{5,4},{6,5},{7,6},{9,8},{10,9},{11,10},{12... | collective-permute-start | bytes 245768 | tf_op jit(solution)/shard_map/ppermute | solution.py:18
  588.6 3.4 copy-start.15
  588.6 3.4 copy-start.30
  588.6 5.5 copy-start.12
  588.6 5.5 copy-start.41
  590.3 4.2 copy-start.8
  590.3 4.2 copy-start.42
  592.0 3.0 copy-start.3
  592.0 3.0 copy-start.45
  592.4 3.0 copy-start.13
  592.4 3.0 copy-start.29
  595.0 1.8 copy-start.4
  595.0 1.8 copy-start.44
  595.9 1.8 copy-start.5
  595.9 1.8 copy-start.39
  596.3 1.8 copy-start.11
  596.3 1.8 copy-start.26
  596.7 1.8 copy-start.1
  596.8 1.8 copy-start.38
  (27 other events, 39.2 us)
